TPU v7x, 128 devices: a whole 4x4x4 slice. The times are simulated.
128 devices in a mesh: row: 8 (over z, core), col: 16 (over y, x).
Axes of the slice: x: 4, y: 4, z: 4, core: 2. Of those that a mesh axis runs over, the one named last changes fastest.
Arguments:
- kernel: bfloat16 [16384, 16384], P('row', 'col'), may hold values from -6 to 6
- labels: int32 [3, 16384], replicated, may hold values from 0 to 63, as said below
Outputs:
- distance: float32 [3, 16384, 64], P(None, ('row', 'col'))
- objective: float32 [3], replicated
Inputs may be any that keep to these rules, and one draw needn't show every extreme that they name: `labels`: in every iteration every cluster of 0 to 63 is named by at least one series.
All inputs are finite; a program needn't handle non-finite values.
Results may differ from a plain program's by a relative error of at most 0.0003.
Values sent between devices are 32-bit elements; how exact they have to be, the bound alone decides.
No kernel may reach another device: no remote copies, remote signals or barrier semaphores. Data moves between devices by JAX's collectives and lax.ppermute only.
A program may use at most 64 MiB of HBM per device.

v0:
```python
import functools

import jax
import jax.numpy as jnp
from jax import lax
from jax.sharding import Mesh
from jax.sharding import PartitionSpec as P

SERIES = 16384
CLUSTERS = 64
ITERS = 3
COL = ("col_0", "col_1")
ROW = ("row_0", "row_1")
ROW_COL = ("row_0", "row_1", "col_0", "col_1")


def cut_along(array, dim, devices):
    before, after = (array.shape[:dim], array.shape[dim + 1 :])
    return jnp.moveaxis(array.reshape(*before, devices, -1, *after), dim, 0)


def summed_on_arrival(array, axis, dim):
    devices = lax.axis_size(axis)
    blocks = lax.all_to_all(cut_along(array, dim, devices), axis, 0, 0, tiled=True)
    return jnp.sum(blocks, axis=0)


def over_axes(array, axes):
    return functools.reduce(lax.psum, axes, array)


def shards(kernel, labels):
    rows_block, cols_block = kernel.shape
    slice_rows = rows_block // lax.axis_size(COL)
    row_base = lax.axis_index(ROW) * rows_block
    col_base = lax.axis_index(COL) * cols_block
    my_offset = lax.axis_index(COL) * slice_rows
    clusters = jnp.arange(CLUSTERS, dtype=jnp.int32)
    col_labels = lax.dynamic_slice_in_dim(labels, col_base, cols_block, 1)
    block_labels = lax.dynamic_slice_in_dim(labels, row_base, rows_block, 1)
    counts = jnp.sum((labels[:, :, None] == clusters).astype(jnp.float32), axis=1)

    def encode(chosen):
        flat = chosen.T[:, :, None] == clusters[None, None, :]
        return flat.reshape(chosen.shape[1], -1).astype(jnp.bfloat16)

    cols_onehot = encode(col_labels)
    sums = summed_on_arrival(
        jnp.dot(kernel, cols_onehot, preferred_element_type=jnp.float32), COL, 0
    )
    mine = lax.dynamic_slice_in_dim(encode(block_labels), my_offset, slice_rows, 0).astype(
        jnp.float32
    )
    totals = over_axes(jnp.sum(mine * sums, axis=0), ROW_COL)
    sums, totals = (sums, totals)
    sums = sums.reshape(slice_rows, ITERS, CLUSTERS).transpose(1, 0, 2)
    totals = totals.reshape(ITERS, CLUSTERS)
    distance = -2.0 * sums / counts[:, None, :] + totals[:, None, :] / (counts * counts)[:, None, :]
    objective = 1.0 - jnp.sum(totals / counts, axis=1) / SERIES
    return (distance, objective)


def solution(mesh):
    finer = Mesh(mesh.devices.reshape(4, 2, 4, 4), ("row_0", "row_1", "col_0", "col_1"))
    return jax.shard_map(
        shards,
        mesh=finer,
        in_specs=(P(ROW, COL), P()),
        out_specs=(P(None, ROW_COL, None), P()),
        check_vma=False,
    )
```

profile of v0, /device:TPU:0, one launch (start us, length us, event | category | flops | bytes accessed | tf_op | source)
XLA Modules:
  0.0 71.1 jit_solution(1358301347358178185)
XLA Ops:
  0.6 0.1 eq.56
  0.7 0.7 %dynamic-slice_bitcast_fusion.1 = s32[1024,3]{0,1:T(4,128)S(1)} fusion(s32[3,16384]{1,0:T(4,128)} %param.3, s32[]{:T(128)S(6)} %select_n.9), kind=kLoop, calls=%fused_computation.11 | loop fusion | bytes 24580 | tf_op jit(solution)/shard_map/transpose | solution.py:44
  1.4 0.2 bitcast_compare_fusion
  1.6 3.7 %convolution_bitcast_fusion = f32[24,16,8,128]{3,2,1,0:T(8,128)S(1)} fusion(pred[1024,192]{0,1:T(32,128)(4,1)S(1)} %bitcast_compare_fusion, bf16[2048,1024]{1,0:T(8,128)(2,1)} %param.2), kind=kOutput, calls=%fused_computation.3 | convolution fusion | flops 805306368 | bytes 5963776 | tf_op jit(solution)/shard_map/dot_general | solution.py:49
  5.3 0.0 copy-start
  5.4 1.3 %copy.9 = f32[24,16,8,128]{3,2,0,1:T(8,128)} copy(f32[24,16,8,128]{3,2,1,0:T(8,128)S(1)} %convolution_bitcast_fusion) | data formatting | bytes 3145728 | tf_op jit(solution)/shard_map/reshape | solution.py:19
  6.7 7.1 %all-to-all-start = ((f32[16,128,192]{1,2,0:T(8,128)}), f32[16,128,192]{1,2,0:T(8,128)S(1)}, u32[]{:S(2)}, u32[]{:S(2)}) async-start(f32[16,128,192]{1,2,0:T(8,128)} %bitcast.17), calls=%async_computation | async-start | bytes 3145728 | tf_op jit(solution)/shard_map/all_to_all | solution.py:24
  13.8 0.0 copy-done
  13.9 1.9 %convert_reduce_fusion = f32[3,64]{1,0:T(4,128)S(1)} fusion(s32[3,16384]{1,0:T(4,128)S(1)} %copy-done), kind=kLoop, calls=%fused_computation | loop fusion | flops 9436992 | bytes 197376 | tf_op jit(solution)/shard_map/reduce_sum | solution.py:41
  15.8 22.5 %all-to-all-done = f32[16,128,192]{1,2,0:T(8,128)S(1)} async-done(((f32[16,128,192]{1,2,0:T(8,128)}), f32[16,128,192]{1,2,0:T(8,128)S(1)}, u32[]{:S(2)}, u32[]{:S(2)}) %all-to-all-start) | async-done | bytes 1572896 | tf_op jit(solution)/shard_map/all_to_all | solution.py:24
  38.3 0.1 reduce_sum.36
  38.4 0.2 eq.62
  38.6 0.2 multiply_reduce_fusion
  38.8 11.8 %psum.28 = f32[192]{0:T(256)S(1)} all-reduce(f32[192]{0:T(256)S(1)} %get-tuple-element.2), channel_id=1, replica_groups=mesh['row_0'=4,'row_1'=2,'col_0'=4,'col_1'=4] {'row_0'}, use_global_device_ids=true, to_apply=%region_3.0 | all-reduce | flops 192 | bytes 1536 | tf_op jit(solution)/shard_map/psum | solution.py:29
  50.6 2.5 %psum.29 = f32[192]{0:T(256)S(1)} all-reduce(f32[192]{0:T(256)S(1)} %psum.28), channel_id=1, replica_groups=mesh['row_0'=4,'row_1'=2,'col_0'=4,'col_1'=4] {'row_1'}, use_global_device_ids=true, to_apply=%region_4.0 | all-reduce | flops 192 | bytes 1536 | tf_op jit(solution)/shard_map/psum | solution.py:29
  53.0 8.8 %psum.30 = f32[192]{0:T(256)S(1)} all-reduce(f32[192]{0:T(256)S(1)} %psum.29), channel_id=1, replica_groups=mesh['row_0'=4,'row_1'=2,'col_0'=4,'col_1'=4] {'col_0'}, use_global_device_ids=true, to_apply=%region_5.0 | all-reduce | flops 192 | bytes 1536 | tf_op jit(solution)/shard_map/psum | solution.py:29
  61.9 0.1 broadcast_in_dim_reshape.3
  61.9 7.7 %psum.31 = f32[3,64]{1,0:T(4,128)S(1)} all-reduce(f32[3,64]{1,0:T(4,128)S(1)} %broadcast_in_dim_reshape.3), channel_id=1, replica_groups=mesh['row_0'=4,'row_1'=2,'col_0'=4,'col_1'=4] {'col_1'}, use_global_device_ids=true, to_apply=%region_6.0 | all-reduce | flops 192 | bytes 1536 | tf_op jit(solution)/shard_map/psum | solution.py:29
  69.7 0.1 divide_reduce_fusion
  69.8 0.5 multiply_subtract_fusion
  70.3 0.8 %add_bitcast_fusion = f32[3,128,64]{1,2,0:T(8,128)} fusion(f32[128,3,64]{0,2,1:T(8,128)S(1)} %bitcast.19, f32[3,64]{1,0:T(4,128)S(1)} %get-tuple-element.5, f32[3,64]{1,0:T(4,128)S(1)} %convert_reduce_fusion), kind=kLoop, calls=%fused_computation.6 | loop fusion | flops 49152 | bytes 198144 | tf_op jit(solution)/shard_map/add | solution.py:58
  (2 shorter events, 0.0 us)
Async XLA Ops:
  5.3 8.5 %copy-start = (s32[3,16384]{1,0:T(4,128)S(1)}, s32[3,16384]{1,0:T(4,128)}, u32[]{:S(2)}) copy-start(s32[3,16384]{1,0:T(4,128)} %param.3) | copy-start | bytes 589828
  6.7 31.7 %all-to-all-start = ((f32[16,128,192]{1,2,0:T(8,128)}), f32[16,128,192]{1,2,0:T(8,128)S(1)}, u32[]{:S(2)}, u32[]{:S(2)}) async-start(f32[16,128,192]{1,2,0:T(8,128)} %bitcast.17), calls=%async_computation | async-start | bytes 3145728 | tf_op jit(solution)/shard_map/all_to_all | solution.py:24
where the time goes:
time: 71.8 us; the launch traced here: 71.1 us
  blocking collectives  30.8 us (43%)
  waiting for transfers between devices  22.5 us (31%)
  starting transfers between devices  7.15 us (10%)
  other arithmetic  3.78 us (5%)
  matrix products  3.71 us (5%)
  local copies, waits for them, and re-layouts  2.38 us (3%)
    psum x4, blocking collectives, over_axes(): return functools.reduce(lax.psum, axes, array)  30.8 us
    all_to_all x1, waiting for transfers between devices, summed_on_arrival(): lax.all_to_all(cut_along(array, dim, devices), axis, 0, 0, tiled=True)  22.5 us
    all_to_all x1, starting transfers between devices, summed_on_arrival(): lax.all_to_all(cut_along(array, dim, devices), axis, 0, 0, tiled=True)  7.15 us
    dot_general x1, matrix products, shards(): jnp.dot(kernel, cols_onehot, preferred_element_type=jnp.float32)  3.71 us
    reduce_sum x1, other arithmetic, shards(): jnp.sum((labels[:, :, None] == clusters).astype(jnp.float32), axis=1)  1.94 us
  transfers between devices with their start and end apart: 1, of which 1 were waited for; matrix products, arithmetic and copies ran while one was open for 3% of the time, Pallas kernels for 0%

commit v1 on v0

--- a/solution.py
+++ b/solution.py
@@ -34,7 +34,6 @@
     slice_rows = rows_block // lax.axis_size(COL)
     row_base = lax.axis_index(ROW) * rows_block
     col_base = lax.axis_index(COL) * cols_block
-    my_offset = lax.axis_index(COL) * slice_rows
     clusters = jnp.arange(CLUSTERS, dtype=jnp.int32)
     col_labels = lax.dynamic_slice_in_dim(labels, col_base, cols_block, 1)
     block_labels = lax.dynamic_slice_in_dim(labels, row_base, rows_block, 1)
@@ -44,15 +43,10 @@
         flat = chosen.T[:, :, None] == clusters[None, None, :]
         return flat.reshape(chosen.shape[1], -1).astype(jnp.bfloat16)
 
-    cols_onehot = encode(col_labels)
-    sums = summed_on_arrival(
-        jnp.dot(kernel, cols_onehot, preferred_element_type=jnp.float32), COL, 0
-    )
-    mine = lax.dynamic_slice_in_dim(encode(block_labels), my_offset, slice_rows, 0).astype(
-        jnp.float32
-    )
-    totals = over_axes(jnp.sum(mine * sums, axis=0), ROW_COL)
-    sums, totals = (sums, totals)
+    partial = jnp.dot(kernel, encode(col_labels), preferred_element_type=jnp.float32)
+    weights = encode(block_labels).astype(jnp.float32)
+    totals = over_axes(jnp.sum(weights * partial, axis=0), ROW_COL)
+    sums = summed_on_arrival(partial, COL, 0)
     sums = sums.reshape(slice_rows, ITERS, CLUSTERS).transpose(1, 0, 2)
     totals = totals.reshape(ITERS, CLUSTERS)
     distance = -2.0 * sums / counts[:, None, :] + totals[:, None, :] / (counts * counts)[:, None, :]

time: 71.8 us -> 54.5 us (0.76)
  waiting for transfers between devices: 22.5 us -> 0.01 us
  blocking collectives: 30.8 us -> 35.4 us
    all_to_all x1, waiting for transfers between devices: 22.5 us -> 0.01 us  [summed_on_arrival(): lax.all_to_all(cut_along(array, dim, devices), axis, 0, 0, tiled=True)]
    psum x4, blocking collectives: 30.8 us -> 35.4 us  [over_axes(): return functools.reduce(lax.psum, axes, array)]
    transpose x2, local copies, waits for them, and re-layouts: 0.73 us -> 1.48 us  [encode(): flat = chosen.T[:, :, None] == clusters[None, None, :]]
  transfers between devices with their start and end apart: 1 -> 1, of which waited for: 1 -> 0; matrix products, arithmetic and copies ran while one was open for 3% -> 5% of each run, Pallas kernels for 0% -> 0%
where the time goes in v1:
time: 54.5 us; the launch traced here: 54.1 us
  blocking collectives  35.4 us (65%)
  starting transfers between devices  7.27 us (13%)
  other arithmetic  3.89 us (7%)
  matrix products  3.82 us (7%)
  local copies, waits for them, and re-layouts  2.98 us (5%)
  between operations  0.69 us (1%)
    psum x4, blocking collectives, over_axes(): return functools.reduce(lax.psum, axes, array)  35.4 us
    all_to_all x1, starting transfers between devices, summed_on_arrival(): lax.all_to_all(cut_along(array, dim, devices), axis, 0, 0, tiled=True)  7.27 us
    dot_general x1, matrix products, shards(): jnp.dot(kernel, encode(col_labels), preferred_element_type=jnp.float32)  3.82 us
    reduce_sum x1, other arithmetic, shards(): jnp.sum((labels[:, :, None] == clusters).astype(jnp.float32), axis=1)  1.94 us
    transpose x2, local copies, waits for them, and re-layouts, encode(): flat = chosen.T[:, :, None] == clusters[None, None, :]  1.48 us
    reshape x1, local copies, waits for them, and re-layouts, cut_along(): return jnp.moveaxis(array.reshape(*before, devices, -1, *after), dim, 0)  1.32 us
  transfers between devices with their start and end apart: 1, of which 0 were waited for; matrix products, arithmetic and copies ran while one was open for 5% of the time, Pallas kernels for 0%

profile of v1, /device:TPU:0, one launch (start us, length us, event | category | flops | bytes accessed | tf_op | source)
XLA Modules:
  0.0 54.1 jit_solution(16189025470498060190)
XLA Ops:
  0.6 0.1 eq.56
  0.7 0.8 %dynamic-slice_bitcast_fusion = s32[2048,3]{0,1:T(4,128)S(1)} fusion(s32[3,16384]{1,0:T(4,128)} %param.3, s32[]{:T(128)S(6)} %select_n.7), kind=kLoop, calls=%fused_computation.9 | loop fusion | bytes 49156 | tf_op jit(solution)/shard_map/transpose | solution.py:43
  1.5 0.7 %dynamic-slice_bitcast_fusion.1 = s32[1024,3]{0,1:T(4,128)S(1)} fusion(s32[3,16384]{1,0:T(4,128)} %param.3, s32[]{:T(128)S(6)} %select_n.6), kind=kLoop, calls=%fused_computation.10 | loop fusion | bytes 24580 | tf_op jit(solution)/shard_map/transpose | solution.py:43
  2.2 0.3 bitcast_compare_fusion
  2.5 0.2 bitcast_compare_fusion.1
  2.7 3.8 %fusion = (f32[192]{0:T(256)S(1)}, f32[192,2048]{1,0:T(8,128)S(1)}) fusion(pred[2048,192]{0,1:T(32,128)(4,1)S(1)} %bitcast_compare_fusion, pred[1024,192]{0,1:T(32,128)(4,1)S(1)} %bitcast_compare_fusion.1, bf16[2048,1024]{1,0:T(8,128)(2,1)} %param.2), kind=kOutput, calls=%fused_computation.5 | convolution fusion | flops 806879040 | bytes 6357760 | tf_op jit(solution)/shard_map/dot_general | solution.py:46
  6.5 1.3 %copy_bitcast_fusion = f32[16,128,192]{1,2,0:T(8,128)} fusion(f32[192,2048]{1,0:T(8,128)S(1)} %get-tuple-element.5), kind=kLoop, calls=%fused_computation.2 | loop fusion | bytes 3145728 | tf_op jit(solution)/shard_map/reshape | solution.py:19
  7.8 0.0 copy-start
  7.8 7.3 %all-to-all-start = ((f32[16,128,192]{1,2,0:T(8,128)}), f32[16,128,192]{1,2,0:T(8,128)S(1)}, u32[]{:S(2)}, u32[]{:S(2)}) async-start(f32[16,128,192]{1,2,0:T(8,128)} %copy_bitcast_fusion), calls=%async_computation | async-start | bytes 3145728 | tf_op jit(solution)/shard_map/all_to_all | solution.py:24
  15.1 11.8 %psum.28 = f32[192]{0:T(256)S(1)} all-reduce(f32[192]{0:T(256)S(1)} %get-tuple-element.4), channel_id=1, replica_groups=mesh['row_0'=4,'row_1'=2,'col_0'=4,'col_1'=4] {'row_0'}, use_global_device_ids=true, to_apply=%region_3.0 | all-reduce | flops 192 | bytes 1536 | tf_op jit(solution)/shard_map/psum | solution.py:29
  26.9 2.5 %psum.29 = f32[192]{0:T(256)S(1)} all-reduce(f32[192]{0:T(256)S(1)} %psum.28), channel_id=1, replica_groups=mesh['row_0'=4,'row_1'=2,'col_0'=4,'col_1'=4] {'row_1'}, use_global_device_ids=true, to_apply=%region_4.0 | all-reduce | flops 192 | bytes 1536 | tf_op jit(solution)/shard_map/psum | solution.py:29
  29.3 10.8 %psum.30 = f32[192]{0:T(256)S(1)} all-reduce(f32[192]{0:T(256)S(1)} %psum.29), channel_id=1, replica_groups=mesh['row_0'=4,'row_1'=2,'col_0'=4,'col_1'=4] {'col_0'}, use_global_device_ids=true, to_apply=%region_5.0 | all-reduce | flops 192 | bytes 1536 | tf_op jit(solution)/shard_map/psum | solution.py:29
  40.2 0.1 broadcast_in_dim_reshape.3
  40.2 10.4 %psum.31 = f32[3,64]{1,0:T(4,128)S(1)} all-reduce(f32[3,64]{1,0:T(4,128)S(1)} %broadcast_in_dim_reshape.3), channel_id=1, replica_groups=mesh['row_0'=4,'row_1'=2,'col_0'=4,'col_1'=4] {'col_1'}, use_global_device_ids=true, to_apply=%region_6.0 | all-reduce | flops 192 | bytes 1536 | tf_op jit(solution)/shard_map/psum | solution.py:29
  50.6 0.0 copy-done
  50.6 1.9 %convert_reduce_fusion = f32[3,64]{1,0:T(4,128)S(1)} fusion(s32[3,16384]{1,0:T(4,128)S(1)} %copy-done), kind=kLoop, calls=%fused_computation | loop fusion | flops 9436992 | bytes 197376 | tf_op jit(solution)/shard_map/reduce_sum | solution.py:40
  52.6 0.1 divide_reduce_fusion
  52.7 0.5 multiply_subtract_fusion
  53.2 0.0 all-to-all-done
  53.2 0.1 reduce_sum.36
  53.3 0.8 %add_bitcast_fusion = f32[3,128,64]{1,2,0:T(8,128)} fusion(f32[128,3,64]{0,2,1:T(8,128)S(1)} %bitcast.22, f32[3,64]{1,0:T(4,128)S(1)} %get-tuple-element.3, f32[3,64]{1,0:T(4,128)S(1)} %convert_reduce_fusion), kind=kLoop, calls=%fused_computation.7 | loop fusion | flops 49152 | bytes 198144 | tf_op jit(solution)/shard_map/add | solution.py:52
  (2 shorter events, 0.0 us)
Async XLA Ops:
  7.8 42.8 %copy-start = (s32[3,16384]{1,0:T(4,128)S(1)}, s32[3,16384]{1,0:T(4,128)}, u32[]{:S(2)}) copy-start(s32[3,16384]{1,0:T(4,128)} %param.3) | copy-start | bytes 589828
  7.8 45.4 %all-to-all-start = ((f32[16,128,192]{1,2,0:T(8,128)}), f32[16,128,192]{1,2,0:T(8,128)S(1)}, u32[]{:S(2)}, u32[]{:S(2)}) async-start(f32[16,128,192]{1,2,0:T(8,128)} %copy_bitcast_fusion), calls=%async_computation | async-start | bytes 3145728 | tf_op jit(solution)/shard_map/all_to_all | solution.py:24

commit v2 on v1

v2 whole, which is shorter than its diff:
```python
import jax
import jax.numpy as jnp
from jax import lax
from jax.experimental import pallas as pl
from jax.experimental.pallas import tpu as pltpu
from jax.sharding import Mesh
from jax.sharding import PartitionSpec as P


SERIES = 16384
CLUSTERS = 64
ITERS = 3
WIDTH = ITERS * CLUSTERS
SLICE = 128
WAVES = ((0, 4), (4, 8), (12, 4))
AXES = ("z", "k", "y", "x")


def index(z, k, y, x):
    return ((z * 2 + k) * 4 + y) * 4 + x


PLACES = [(z, k, y, x) for z in range(4) for k in range(2) for y in range(4) for x in range(4)]


def first_stage(d):
    return [(index(z, k, y, x), index(z, k, y ^ (d * k), x ^ (d * (1 - k)))) for z, k, y, x in PLACES]


def second_stage(d):
    return [(index(z, k, y, x), index(z, k, y ^ (d * (1 - k)), x ^ (d * k))) for z, k, y, x in PLACES]


def partial_sums(place, kernel, labels, *refs):
    parts, totals = refs[:4], refs[4]
    held, cols, rows, sems = refs[5:]
    depth = cols.shape[1]
    zk, at = place[0] // 16, place[0] % 16
    k, y, x = zk % 2, at // 4, at % 4
    starts = []
    for d in range(4):
        for e in range(4):
            outer, inner = y ^ jnp.where(k == 0, e, d), x ^ jnp.where(k == 0, d, e)
            starts.append(pl.multiple_of((outer * 4 + inner) * SLICE, SLICE))
    row_base = pl.multiple_of(zk * rows.shape[1], SLICE)
    col_base = pl.multiple_of(at * depth, SLICE)
    copies = [
        pltpu.make_async_copy(labels.at[:, pl.ds(col_base, cols.shape[1])], cols, sems.at[16]),
        pltpu.make_async_copy(labels.at[:, pl.ds(row_base, rows.shape[1])], rows, sems.at[17]),
    ]
    blocks = []
    for step in range(16):
        blocks.append(
            pltpu.make_async_copy(kernel.at[pl.ds(starts[step], SLICE), :], held.at[step], sems.at[step])
        )
    for copy in copies + blocks:
        copy.start()
    copies[0].wait()
    wide = lax.broadcasted_iota(jnp.int32, (CLUSTERS, depth), 0)
    onehot = jnp.concatenate(
        [(wide == cols[t : t + 1, :]).astype(jnp.float32).astype(jnp.bfloat16) for t in range(ITERS)]
    )
    copies[1].wait()
    narrow = lax.broadcasted_iota(jnp.int32, (CLUSTERS, SLICE), 0)
    sums = [jnp.zeros((CLUSTERS, SLICE), jnp.float32) for _ in range(ITERS)]
    for step, size in WAVES:
        for one in range(step, step + size):
            blocks[one].wait()
        wave = lax.dot_general(
            onehot,
            held[step : step + size].reshape(size * SLICE, depth),
            (((1,), (1,)), ((), ())),
            preferred_element_type=jnp.float32,
        )
        for one in range(step, step + size):
            part = wave[:, (one - step) * SLICE : (one - step + 1) * SLICE]
            parts[one // 4][one % 4] = part
            for t in range(ITERS):
                chosen = narrow == rows[t : t + 1, pl.ds(starts[one], SLICE)]
                sums[t] += jnp.where(chosen, part[t * CLUSTERS : (t + 1) * CLUSTERS], 0.0)
    lines = [jnp.sum(a.T, axis=0, keepdims=True) for a in sums]
    lines.append(jnp.zeros((1, CLUSTERS), jnp.float32))
    both = jnp.concatenate([jnp.concatenate(lines[0:4:2]), jnp.concatenate(lines[1:4:2])], axis=1)
    totals[...] = jnp.broadcast_to(both, totals.shape)


def stage_sum(a, b, c, d, *outs):
    for e in range(4):
        outs[e][...] = (a[e] + b[e]) + (c[e] + d[e])


def tally(labels, after, counts):
    del after
    octet = lax.broadcasted_iota(jnp.int32, (8, SERIES), 0)
    spread = lax.broadcasted_iota(jnp.int32, (8, CLUSTERS), 1) // 8
    keep = spread == lax.broadcasted_iota(jnp.int32, (8, CLUSTERS), 0)
    for t in range(ITERS):
        line = labels[t : t + 1, :]
        high = (octet == line >> 3).astype(jnp.float32).astype(jnp.bfloat16)
        low = (octet == (line & 7)).astype(jnp.float32).astype(jnp.bfloat16)
        square = lax.dot_general(
            high, low, (((1,), (1,)), ((), ())), preferred_element_type=jnp.float32
        )
        row = jnp.sum(jnp.where(keep, jnp.concatenate([square] * 8, axis=1), 0.0), axis=0, keepdims=True)
        counts[t] = jnp.broadcast_to(row, (SLICE, CLUSTERS)).T


def finish(a, b, c, d, counts, shares, distance, objective):
    sums = (a[...] + b[...]) + (c[...] + d[...])
    whole = jnp.sum(shares[...], axis=0)
    whole = (whole[0:2] + whole[2:4]) + (whole[4:6] + whole[6:8])
    for t in range(ITERS):
        row = whole[t // 2 : t // 2 + 1, t % 2 * CLUSTERS : (t % 2 + 1) * CLUSTERS]
        totals = jnp.broadcast_to(row, (SLICE, CLUSTERS)).T
        count = counts[t]
        block = sums[t * CLUSTERS : (t + 1) * CLUSTERS]
        distance[t] = (-2.0 * block) / count + totals / (count * count)
        objective[t] = 1.0 - jnp.sum((totals / count)[:, 0:1]) / SERIES


def near(array):
    return pltpu.with_memory_space_constraint(array, pltpu.VMEM)


def vmem():
    return pl.BlockSpec(memory_space=pltpu.VMEM)


def shards(kernel, labels):
    rows_block, cols_block = kernel.shape
    place = lax.axis_index(AXES).reshape(1).astype(jnp.int32)
    block = pltpu.VMEM((4, WIDTH, SLICE), jnp.float32)
    small = pltpu.VMEM((WIDTH, SLICE), jnp.float32)
    *parts, totals = pl.pallas_call(
        partial_sums,
        out_shape=[block] * 4 + [pltpu.VMEM((len(PLACES), 2, SLICE), jnp.float32)],
        in_specs=[
            pl.BlockSpec(memory_space=pltpu.SMEM),
            pl.BlockSpec(memory_space=pl.ANY),
            pl.BlockSpec(memory_space=pl.ANY),
        ],
        out_specs=[vmem()] * 5,
        scratch_shapes=[
            pltpu.VMEM((16, SLICE, cols_block), jnp.bfloat16),
            pltpu.VMEM((ITERS, cols_block), jnp.int32),
            pltpu.VMEM((ITERS, rows_block), jnp.int32),
            pltpu.SemaphoreType.DMA((18,)),
        ],
    )(place, kernel, labels)
    moved = [parts[0]] + [lax.ppermute(parts[s], AXES, first_stage(s)) for s in (1, 3, 2)]
    halves = pl.pallas_call(
        stage_sum, out_shape=[small] * 4, in_specs=[vmem()] * 4, out_specs=[vmem()] * 4
    )(*map(near, moved))
    last = [halves[0]]
    for s in (2, 1, 3):
        last.append(lax.ppermute(halves[s], AXES, second_stage(s)))
    counts = pl.pallas_call(
        tally,
        out_shape=pltpu.VMEM((ITERS, CLUSTERS, SLICE), jnp.float32),
        in_specs=[vmem()] * 2,
        out_specs=vmem(),
    )(labels, near(halves[0]))
    shares = lax.all_to_all(totals, AXES, 0, 0, tiled=True)
    shares = shares.reshape(len(PLACES) // 4, 8, SLICE)
    distance, objective = pl.pallas_call(
        finish,
        out_shape=[
            jax.ShapeDtypeStruct((ITERS, CLUSTERS, SLICE), jnp.float32),
            jax.ShapeDtypeStruct((ITERS,), jnp.float32),
        ],
        in_specs=[vmem()] * 6,
        out_specs=[vmem(), pl.BlockSpec(memory_space=pltpu.SMEM)],
    )(*map(near, last), near(counts), near(shares))
    return jnp.swapaxes(distance, 1, 2), objective


def solution(mesh):
    finer = Mesh(mesh.devices.reshape(4, 2, 4, 4), AXES)
    return jax.shard_map(
        shards,
        mesh=finer,
        in_specs=(P(("z", "k"), ("y", "x")), P()),
        out_specs=(P(None, AXES, None), P()),
        check_vma=False,
    )
```

time: 54.5 us -> 31.9 us (0.59)
  the two profiles are of different devices: /device:TPU:0 before, /device:TPU:1 now
where the time goes in v2:
time: 31.9 us; the launch traced here: 31.7 us
  starting transfers between devices  19.5 us (61%)
  Pallas kernels  7.06 us (22%)
  waiting for transfers between devices  4.43 us (14%)
  between operations  0.7 us (2%)
    all_to_all x1, starting transfers between devices, shards(): shares = lax.all_to_all(totals, AXES, 0, 0, tiled=True)  10.8 us
    ppermute x3, starting transfers between devices, shards(): lax.ppermute(parts[s], AXES, first_stage(s))  4.83 us
    all_to_all x1, waiting for transfers between devices, shards(): shares = lax.all_to_all(totals, AXES, 0, 0, tiled=True)  4.42 us
    pallas_call x1, Pallas kernels, shards(): pl.pallas_call(partial_sums, out_shape=[block] * 4 + [pltpu.VMEM((len(PLA...  4.2 us
    ppermute x3, starting transfers between devices, shards(): last.append(lax.ppermute(halves[s], AXES, second_stage(s)))  3.83 us
    pallas_call x1, Pallas kernels, shards(): pl.pallas_call(tally, out_shape=pltpu.VMEM((ITERS, CLUSTERS, SLICE), jnp....  1.91 us
    pallas_call x1, Pallas kernels, shards(): pl.pallas_call(finish, out_shape=[jax.ShapeDtypeStruct((ITERS, CLUSTERS,...  0.88 us
  transfers between devices with their start and end apart: 7, of which 1 were waited for; matrix products, arithmetic and copies ran while one was open for 0% of the time, Pallas kernels for 6%

profile of v2, /device:TPU:1, one launch (start us, length us, event | category | flops | bytes accessed | tf_op | source)
XLA Modules:
  0.0 31.7 jit_solution(13172071900448682932)
XLA Ops:
  0.6 4.2 %shard_map.41 = (f32[4,192,128]{2,1,0:T(8,128)S(1)}, f32[4,192,128]{2,1,0:T(8,128)S(1)}, f32[4,192,128]{2,1,0:T(8,128)S(1)}, f32[4,192,128]{2,1,0:T(8,128)S(1)}, f32[128,2,128]{2,1,0:T(2,128)}) custom-call(s32[1]{0:T(128)} %bitcast.place, bf16[2048,1024]{1,0:T(8,128)(2,1)} %kernel.1, s32[3,16384]{1,0:T(4,128)} %labels.3), custom_call_target="tpu_custom_call" | custom-call | tf_op jit(solution)/shard_map/pallas_call | solution.py:134
  4.8 2.2 %collective-permute-start = (f32[4,192,128]{2,1,0:T(8,128)S(1)}, f32[4,192,128]{2,1,0:T(8,128)S(1)}, u32[]{:S(2)}, u32[]{:S(2)}) collective-permute-start(f32[4,192,128]{2,1,0:T(8,128)S(1)} %get-tuple-element.14), channel_id=1, source_target_pairs={{0,1},{1,0},{2,3},{3,2},{4,5},{5,4},{6,7},{7,6},{8,9},{9,8},{10,11... | collective-permute-start | bytes 1179656 | tf_op jit(solution)/shard_map/ppermute | solution.py:150
  7.0 1.9 %collective-permute-start.1 = (f32[4,192,128]{2,1,0:T(8,128)S(1)}, f32[4,192,128]{2,1,0:T(8,128)S(1)}, u32[]{:S(2)}, u32[]{:S(2)}) collective-permute-start(f32[4,192,128]{2,1,0:T(8,128)S(1)} %get-tuple-element.15), channel_id=1, source_target_pairs={{0,3},{1,2},{2,1},{3,0},{4,7},{5,6},{6,5},{7,4},{8,11},{9,10},{10,... | collective-permute-start | bytes 1179656 | tf_op jit(solution)/shard_map/ppermute | solution.py:150
  8.9 0.7 %collective-permute-start.2 = (f32[4,192,128]{2,1,0:T(8,128)S(1)}, f32[4,192,128]{2,1,0:T(8,128)S(1)}, u32[]{:S(2)}, u32[]{:S(2)}) collective-permute-start(f32[4,192,128]{2,1,0:T(8,128)S(1)} %get-tuple-element.16), channel_id=1, source_target_pairs={{0,2},{1,3},{2,0},{3,1},{4,6},{5,7},{6,4},{7,5},{8,10},{9,11},{10,... | collective-permute-start | bytes 1179656 | tf_op jit(solution)/shard_map/ppermute | solution.py:150
  9.7 10.8 %all-to-all-start = ((f32[128,2,128]{2,1,0:T(2,128)}), f32[128,2,128]{2,1,0:T(2,128)S(1)}, u32[]{:S(2)}, u32[]{:S(2)}) async-start(f32[128,2,128]{2,1,0:T(2,128)} %get-tuple-element.21), calls=%async_computation | async-start | bytes 262144 | tf_op jit(solution)/shard_map/all_to_all | solution.py:163
  20.5 0.0 collective-permute-done.b
  20.5 0.0 collective-permute-done.1.c
  20.5 0.0 collective-permute-done.2.d
  20.6 0.1 shard_map.42
  20.6 2.9 %collective-permute-start.3 = (f32[192,128]{1,0:T(8,128)S(1)}, f32[192,128]{1,0:T(8,128)S(1)}, u32[]{:S(2)}, u32[]{:S(2)}) collective-permute-start(f32[192,128]{1,0:T(8,128)S(1)} %get-tuple-element.18), channel_id=1, source_target_pairs={{0,8},{1,9},{2,10},{3,11},{4,12},{5,13},{6,14},{7,15},{8,0},{9,1},... | collective-permute-start | bytes 294920 | tf_op jit(solution)/shard_map/ppermute | solution.py:156
  23.6 0.3 collective-permute-start.4
  23.9 0.6 %collective-permute-start.5 = (f32[192,128]{1,0:T(8,128)S(1)}, f32[192,128]{1,0:T(8,128)S(1)}, u32[]{:S(2)}, u32[]{:S(2)}) collective-permute-start(f32[192,128]{1,0:T(8,128)S(1)} %get-tuple-element.20), channel_id=1, source_target_pairs={{0,12},{1,13},{2,14},{3,15},{4,8},{5,9},{6,10},{7,11},{8,4},{9,5},... | collective-permute-start | bytes 294920 | tf_op jit(solution)/shard_map/ppermute | solution.py:156
  24.5 1.9 %shard_map.43.counts = f32[3,64,128]{2,1,0:T(8,128)S(1)} custom-call(s32[3,16384]{1,0:T(4,128)} %labels.3, f32[192,128]{1,0:T(8,128)S(1)} %get-tuple-element.17.after.a), custom_call_target="tpu_custom_call" | custom-call | tf_op jit(solution)/shard_map/pallas_call | solution.py:157
  26.4 4.4 %all-to-all-done = f32[128,2,128]{2,1,0:T(2,128)S(1)} async-done(((f32[128,2,128]{2,1,0:T(2,128)}), f32[128,2,128]{2,1,0:T(2,128)S(1)}, u32[]{:S(2)}, u32[]{:S(2)}) %all-to-all-start) | async-done | bytes 131104 | tf_op jit(solution)/shard_map/all_to_all | solution.py:163
  30.8 0.0 collective-permute-done.3.b
  30.8 0.0 collective-permute-done.4.c
  30.8 0.0 collective-permute-done.5.d
  30.8 0.9 %shard_map.44 = (f32[3,64,128]{2,1,0:T(8,128)}, f32[3]{0:T(128)}) custom-call(f32[192,128]{1,0:T(8,128)S(1)} %get-tuple-element.17.after.a, f32[192,128]{1,0:T(8,128)S(1)} %collective-permute-done.3.b, f32[192,128]{1,0:T(8,128)S(1)} %collective-permute-done.4.c, f32[192,128]{1,0:T(8,128)S(1)} %collective-permute-done.5.d, ...), custom_call_target="tpu_custom_call" | custom-call | tf_op jit(solution)/shard_map/pallas_call | solution.py:165
Async XLA Ops:
  4.8 15.7 %collective-permute-start = (f32[4,192,128]{2,1,0:T(8,128)S(1)}, f32[4,192,128]{2,1,0:T(8,128)S(1)}, u32[]{:S(2)}, u32[]{:S(2)}) collective-permute-start(f32[4,192,128]{2,1,0:T(8,128)S(1)} %get-tuple-element.14), channel_id=1, source_target_pairs={{0,1},{1,0},{2,3},{3,2},{4,5},{5,4},{6,7},{7,6},{8,9},{9,8},{10,11... | collective-permute-start | bytes 1179656 | tf_op jit(solution)/shard_map/ppermute | solution.py:150
  7.0 13.5 %collective-permute-start.1 = (f32[4,192,128]{2,1,0:T(8,128)S(1)}, f32[4,192,128]{2,1,0:T(8,128)S(1)}, u32[]{:S(2)}, u32[]{:S(2)}) collective-permute-start(f32[4,192,128]{2,1,0:T(8,128)S(1)} %get-tuple-element.15), channel_id=1, source_target_pairs={{0,3},{1,2},{2,1},{3,0},{4,7},{5,6},{6,5},{7,4},{8,11},{9,10},{10,... | collective-permute-start | bytes 1179656 | tf_op jit(solution)/shard_map/ppermute | solution.py:150
  8.9 11.6 %collective-permute-start.2 = (f32[4,192,128]{2,1,0:T(8,128)S(1)}, f32[4,192,128]{2,1,0:T(8,128)S(1)}, u32[]{:S(2)}, u32[]{:S(2)}) collective-permute-start(f32[4,192,128]{2,1,0:T(8,128)S(1)} %get-tuple-element.16), channel_id=1, source_target_pairs={{0,2},{1,3},{2,0},{3,1},{4,6},{5,7},{6,4},{7,5},{8,10},{9,11},{10,... | collective-permute-start | bytes 1179656 | tf_op jit(solution)/shard_map/ppermute | solution.py:150
  9.7 21.1 %all-to-all-start = ((f32[128,2,128]{2,1,0:T(2,128)}), f32[128,2,128]{2,1,0:T(2,128)S(1)}, u32[]{:S(2)}, u32[]{:S(2)}) async-start(f32[128,2,128]{2,1,0:T(2,128)} %get-tuple-element.21), calls=%async_computation | async-start | bytes 262144 | tf_op jit(solution)/shard_map/all_to_all | solution.py:163
  20.6 10.2 %collective-permute-start.3 = (f32[192,128]{1,0:T(8,128)S(1)}, f32[192,128]{1,0:T(8,128)S(1)}, u32[]{:S(2)}, u32[]{:S(2)}) collective-permute-start(f32[192,128]{1,0:T(8,128)S(1)} %get-tuple-element.18), channel_id=1, source_target_pairs={{0,8},{1,9},{2,10},{3,11},{4,12},{5,13},{6,14},{7,15},{8,0},{9,1},... | collective-permute-start | bytes 294920 | tf_op jit(solution)/shard_map/ppermute | solution.py:156
  23.6 7.2 %collective-permute-start.4 = (f32[192,128]{1,0:T(8,128)S(1)}, f32[192,128]{1,0:T(8,128)S(1)}, u32[]{:S(2)}, u32[]{:S(2)}) collective-permute-start(f32[192,128]{1,0:T(8,128)S(1)} %get-tuple-element.19), channel_id=1, source_target_pairs={{0,4},{1,5},{2,6},{3,7},{4,0},{5,1},{6,2},{7,3},{8,12},{9,13},{10,... | collective-permute-start | bytes 294920 | tf_op jit(solution)/shard_map/ppermute | solution.py:156
  23.9 6.9 %collective-permute-start.5 = (f32[192,128]{1,0:T(8,128)S(1)}, f32[192,128]{1,0:T(8,128)S(1)}, u32[]{:S(2)}, u32[]{:S(2)}) collective-permute-start(f32[192,128]{1,0:T(8,128)S(1)} %get-tuple-element.20), channel_id=1, source_target_pairs={{0,12},{1,13},{2,14},{3,15},{4,8},{5,9},{6,10},{7,11},{8,4},{9,5},... | collective-permute-start | bytes 294920 | tf_op jit(solution)/shard_map/ppermute | solution.py:156

commit v3 on v2

--- a/solution.py
+++ b/solution.py
@@ -81,7 +81,7 @@
     lines = [jnp.sum(a.T, axis=0, keepdims=True) for a in sums]
     lines.append(jnp.zeros((1, CLUSTERS), jnp.float32))
     both = jnp.concatenate([jnp.concatenate(lines[0:4:2]), jnp.concatenate(lines[1:4:2])], axis=1)
-    totals[...] = jnp.broadcast_to(both, totals.shape)
+    totals[...] = both
 
 
 def stage_sum(a, b, c, d, *outs):
@@ -122,6 +122,10 @@
     return pltpu.with_memory_space_constraint(array, pltpu.VMEM)
 
 
+def early(part, s):
+    return lax.ppermute(part, AXES, first_stage(s))
+
+
 def vmem():
     return pl.BlockSpec(memory_space=pltpu.VMEM)
 
@@ -133,7 +137,7 @@
     small = pltpu.VMEM((WIDTH, SLICE), jnp.float32)
     *parts, totals = pl.pallas_call(
         partial_sums,
-        out_shape=[block] * 4 + [pltpu.VMEM((len(PLACES), 2, SLICE), jnp.float32)],
+        out_shape=[block] * 4 + [pltpu.VMEM((2, SLICE), jnp.float32)],
         in_specs=[
             pl.BlockSpec(memory_space=pltpu.SMEM),
             pl.BlockSpec(memory_space=pl.ANY),
@@ -147,12 +151,14 @@
             pltpu.SemaphoreType.DMA((18,)),
         ],
     )(place, kernel, labels)
-    moved = [parts[0]] + [lax.ppermute(parts[s], AXES, first_stage(s)) for s in (1, 3, 2)]
+    other = lax.ppermute(totals, "k", [(0, 1), (1, 0)])
+    chip = totals + other
+    moved = [parts[0]] + [early(parts[s], s) for s in (1, 3, 2)]
     halves = pl.pallas_call(
         stage_sum, out_shape=[small] * 4, in_specs=[vmem()] * 4, out_specs=[vmem()] * 4
     )(*map(near, moved))
     last = [halves[0]]
-    for s in (2, 1, 3):
+    for s in (2, 3, 1):
         last.append(lax.ppermute(halves[s], AXES, second_stage(s)))
     counts = pl.pallas_call(
         tally,
@@ -160,8 +166,10 @@
         in_specs=[vmem()] * 2,
         out_specs=vmem(),
     )(labels, near(halves[0]))
-    shares = lax.all_to_all(totals, AXES, 0, 0, tiled=True)
-    shares = shares.reshape(len(PLACES) // 4, 8, SLICE)
+    shares = lax.all_to_all(
+        jnp.broadcast_to(chip[None], (64, 2, SLICE)), ("z", "y", "x"), 0, 0, tiled=True
+    )
+    shares = shares.reshape(16, 8, SLICE)
     distance, objective = pl.pallas_call(
         finish,
         out_shape=[

time: 31.9 us -> 46.9 us (1.47)
  the two profiles are of different devices: /device:TPU:1 before, /device:TPU:0 now
where the time goes in v3:
time: 46.9 us; the launch traced here: 46.7 us
  starting transfers between devices  19.7 us (42%)
  waiting for transfers between devices  19.3 us (41%)
  Pallas kernels  6.37 us (14%)
  between operations  0.68 us (1%)
  local copies, waits for them, and re-layouts  0.65 us (1%)
    all_to_all x1, starting transfers between devices, shards(): lax.all_to_all(jnp.broadcast_to(chip[None], (64, 2, SLICE)), ('z', 'y', '...  10.9 us
    ppermute x3, waiting for transfers between devices, early(): return lax.ppermute(part, AXES, first_stage(s))  10.5 us
    all_to_all x1, waiting for transfers between devices, shards(): lax.all_to_all(jnp.broadcast_to(chip[None], (64, 2, SLICE)), ('z', 'y', '...  7.67 us
    ppermute x3, starting transfers between devices, early(): return lax.ppermute(part, AXES, first_stage(s))  4.43 us
    ppermute x3, starting transfers between devices, shards(): last.append(lax.ppermute(halves[s], AXES, second_stage(s)))  4.33 us
    pallas_call x1, Pallas kernels, shards(): pl.pallas_call(partial_sums, out_shape=[block] * 4 + [pltpu.VMEM((2, SLIC...  3.52 us
    pallas_call x1, Pallas kernels, shards(): pl.pallas_call(tally, out_shape=pltpu.VMEM((ITERS, CLUSTERS, SLICE), jnp....  1.91 us
    ppermute x1, waiting for transfers between devices, shards(): other = lax.ppermute(totals, 'k', [(0, 1), (1, 0)])  1.16 us
  transfers between devices with their start and end apart: 8, of which 4 were waited for; matrix products, arithmetic and copies ran while one was open for 1% of the time, Pallas kernels for 4%

profile of v3, /device:TPU:0, one launch (start us, length us, event | category | flops | bytes accessed | tf_op | source)
XLA Modules:
  0.0 46.7 jit_solution(9426905091050625257)
XLA Ops:
  0.6 3.5 %shard_map.41 = (f32[4,192,128]{2,1,0:T(8,128)S(1)}, f32[4,192,128]{2,1,0:T(8,128)S(1)}, f32[4,192,128]{2,1,0:T(8,128)S(1)}, f32[4,192,128]{2,1,0:T(8,128)S(1)}, f32[2,128]{1,0:T(2,128)S(1)}) custom-call(s32[1]{0:T(128)} %bitcast.place, bf16[2048,1024]{1,0:T(8,128)(2,1)} %kernel.1, s32[3,16384]{1,0:T(4,128)} %labels.3), custom_call_target="tpu_custom_call" | custom-call | tf_op jit(solution)/shard_map/pallas_call | solution.py:138
  4.2 1.7 %collective-permute-start = (f32[4,192,128]{2,1,0:T(8,128)S(1)}, f32[4,192,128]{2,1,0:T(8,128)S(1)}, u32[]{:S(2)}, u32[]{:S(2)}) collective-permute-start(f32[4,192,128]{2,1,0:T(8,128)S(1)} %get-tuple-element.14), channel_id=1, source_target_pairs={{0,1},{1,0},{2,3},{3,2},{4,5},{5,4},{6,7},{7,6},{8,9},{9,8},{10,11... | collective-permute-start | bytes 1179656 | tf_op jit(solution)/shard_map/ppermute | solution.py:126
  5.9 2.1 %collective-permute-start.1 = (f32[4,192,128]{2,1,0:T(8,128)S(1)}, f32[4,192,128]{2,1,0:T(8,128)S(1)}, u32[]{:S(2)}, u32[]{:S(2)}) collective-permute-start(f32[4,192,128]{2,1,0:T(8,128)S(1)} %get-tuple-element.15), channel_id=1, source_target_pairs={{0,3},{1,2},{2,1},{3,0},{4,7},{5,6},{6,5},{7,4},{8,11},{9,10},{10,... | collective-permute-start | bytes 1179656 | tf_op jit(solution)/shard_map/ppermute | solution.py:126
  8.0 0.6 %collective-permute-start.2 = (f32[4,192,128]{2,1,0:T(8,128)S(1)}, f32[4,192,128]{2,1,0:T(8,128)S(1)}, u32[]{:S(2)}, u32[]{:S(2)}) collective-permute-start(f32[4,192,128]{2,1,0:T(8,128)S(1)} %get-tuple-element.16), channel_id=1, source_target_pairs={{0,2},{1,3},{2,0},{3,1},{4,6},{5,7},{6,4},{7,5},{8,10},{9,11},{10,... | collective-permute-start | bytes 1179656 | tf_op jit(solution)/shard_map/ppermute | solution.py:126
  8.6 3.4 %collective-permute-done.b = f32[4,192,128]{2,1,0:T(8,128)S(1)} collective-permute-done((f32[4,192,128]{2,1,0:T(8,128)S(1)}, f32[4,192,128]{2,1,0:T(8,128)S(1)}, u32[]{:S(2)}, u32[]{:S(2)}) %collective-permute-start) | collective-permute-done | bytes 393248 | tf_op jit(solution)/shard_map/ppermute | solution.py:126
  12.0 7.0 %collective-permute-done.1.c = f32[4,192,128]{2,1,0:T(8,128)S(1)} collective-permute-done((f32[4,192,128]{2,1,0:T(8,128)S(1)}, f32[4,192,128]{2,1,0:T(8,128)S(1)}, u32[]{:S(2)}, u32[]{:S(2)}) %collective-permute-start.1) | collective-permute-done | bytes 393248 | tf_op jit(solution)/shard_map/ppermute | solution.py:126
  19.1 0.0 collective-permute-done.2.d
  19.1 0.1 shard_map.42
  19.1 3.3 %collective-permute-start.3 = (f32[192,128]{1,0:T(8,128)S(1)}, f32[192,128]{1,0:T(8,128)S(1)}, u32[]{:S(2)}, u32[]{:S(2)}) collective-permute-start(f32[192,128]{1,0:T(8,128)S(1)} %get-tuple-element.18), channel_id=1, source_target_pairs={{0,8},{1,9},{2,10},{3,11},{4,12},{5,13},{6,14},{7,15},{8,0},{9,1},... | collective-permute-start | bytes 294920 | tf_op jit(solution)/shard_map/ppermute | solution.py:162
  22.4 1.1 %collective-permute-start.4 = (f32[192,128]{1,0:T(8,128)S(1)}, f32[192,128]{1,0:T(8,128)S(1)}, u32[]{:S(2)}, u32[]{:S(2)}) collective-permute-start(f32[192,128]{1,0:T(8,128)S(1)} %get-tuple-element.19), channel_id=1, source_target_pairs={{0,12},{1,13},{2,14},{3,15},{4,8},{5,9},{6,10},{7,11},{8,4},{9,5},... | collective-permute-start | bytes 294920 | tf_op jit(solution)/shard_map/ppermute | solution.py:162
  23.5 0.0 collective-permute-start.5
  23.5 0.0 collective-permute-start.6
  23.5 1.2 %collective-permute-done.6 = f32[2,128]{1,0:T(2,128)S(1)} collective-permute-done((f32[2,128]{1,0:T(2,128)S(1)}, f32[2,128]{1,0:T(2,128)S(1)}, u32[]{:S(2)}, u32[]{:S(2)}) %collective-permute-start.6) | collective-permute-done | bytes 1056 | tf_op jit(solution)/shard_map/ppermute | solution.py:154
  24.6 0.7 %broadcast_in_dim.2 = f32[64,2,128]{2,1,0:T(2,128)} broadcast(f32[2,128]{1,0:T(2,128)S(1)} %add.15), dimensions={1,2} | broadcast | bytes 66560 | tf_op jit(solution)/shard_map/broadcast_in_dim | solution.py:170
  25.3 10.9 %all-to-all-start = ((f32[64,2,128]{2,1,0:T(2,128)}), f32[64,2,128]{2,1,0:T(2,128)S(1)}, u32[]{:S(2)}, u32[]{:S(2)}) async-start(f32[64,2,128]{2,1,0:T(2,128)} %broadcast_in_dim.2), calls=%async_computation | async-start | bytes 131072 | tf_op jit(solution)/shard_map/all_to_all | solution.py:169
  36.2 1.9 %shard_map.43.counts = f32[3,64,128]{2,1,0:T(8,128)S(1)} custom-call(s32[3,16384]{1,0:T(4,128)} %labels.3, f32[192,128]{1,0:T(8,128)S(1)} %get-tuple-element.17.after.a), custom_call_target="tpu_custom_call" | custom-call | tf_op jit(solution)/shard_map/pallas_call | solution.py:163
  38.2 7.7 %all-to-all-done = f32[64,2,128]{2,1,0:T(2,128)S(1)} async-done(((f32[64,2,128]{2,1,0:T(2,128)}), f32[64,2,128]{2,1,0:T(2,128)S(1)}, u32[]{:S(2)}, u32[]{:S(2)}) %all-to-all-start) | async-done | bytes 65568 | tf_op jit(solution)/shard_map/all_to_all | solution.py:169
  45.8 0.0 collective-permute-done.3.b
  45.8 0.0 collective-permute-done.4.c
  45.8 0.0 collective-permute-done.5.d
  45.8 0.9 %shard_map.44 = (f32[3,64,128]{2,1,0:T(8,128)}, f32[3]{0:T(128)}) custom-call(f32[192,128]{1,0:T(8,128)S(1)} %get-tuple-element.17.after.a, f32[192,128]{1,0:T(8,128)S(1)} %collective-permute-done.3.b, f32[192,128]{1,0:T(8,128)S(1)} %collective-permute-done.4.c, f32[192,128]{1,0:T(8,128)S(1)} %collective-permute-done.5.d, ...), custom_call_target="tpu_custom_call" | custom-call | tf_op jit(solution)/shard_map/pallas_call | solution.py:173
  (1 shorter events, 0.0 us)
Async XLA Ops:
  4.2 7.9 %collective-permute-start = (f32[4,192,128]{2,1,0:T(8,128)S(1)}, f32[4,192,128]{2,1,0:T(8,128)S(1)}, u32[]{:S(2)}, u32[]{:S(2)}) collective-permute-start(f32[4,192,128]{2,1,0:T(8,128)S(1)} %get-tuple-element.14), channel_id=1, source_target_pairs={{0,1},{1,0},{2,3},{3,2},{4,5},{5,4},{6,7},{7,6},{8,9},{9,8},{10,11... | collective-permute-start | bytes 1179656 | tf_op jit(solution)/shard_map/ppermute | solution.py:126
  5.9 13.2 %collective-permute-start.1 = (f32[4,192,128]{2,1,0:T(8,128)S(1)}, f32[4,192,128]{2,1,0:T(8,128)S(1)}, u32[]{:S(2)}, u32[]{:S(2)}) collective-permute-start(f32[4,192,128]{2,1,0:T(8,128)S(1)} %get-tuple-element.15), channel_id=1, source_target_pairs={{0,3},{1,2},{2,1},{3,0},{4,7},{5,6},{6,5},{7,4},{8,11},{9,10},{10,... | collective-permute-start | bytes 1179656 | tf_op jit(solution)/shard_map/ppermute | solution.py:126
  8.0 11.1 %collective-permute-start.2 = (f32[4,192,128]{2,1,0:T(8,128)S(1)}, f32[4,192,128]{2,1,0:T(8,128)S(1)}, u32[]{:S(2)}, u32[]{:S(2)}) collective-permute-start(f32[4,192,128]{2,1,0:T(8,128)S(1)} %get-tuple-element.16), channel_id=1, source_target_pairs={{0,2},{1,3},{2,0},{3,1},{4,6},{5,7},{6,4},{7,5},{8,10},{9,11},{10,... | collective-permute-start | bytes 1179656 | tf_op jit(solution)/shard_map/ppermute | solution.py:126
  19.1 26.7 %collective-permute-start.3 = (f32[192,128]{1,0:T(8,128)S(1)}, f32[192,128]{1,0:T(8,128)S(1)}, u32[]{:S(2)}, u32[]{:S(2)}) collective-permute-start(f32[192,128]{1,0:T(8,128)S(1)} %get-tuple-element.18), channel_id=1, source_target_pairs={{0,8},{1,9},{2,10},{3,11},{4,12},{5,13},{6,14},{7,15},{8,0},{9,1},... | collective-permute-start | bytes 294920 | tf_op jit(solution)/shard_map/ppermute | solution.py:162
  22.4 23.4 %collective-permute-start.4 = (f32[192,128]{1,0:T(8,128)S(1)}, f32[192,128]{1,0:T(8,128)S(1)}, u32[]{:S(2)}, u32[]{:S(2)}) collective-permute-start(f32[192,128]{1,0:T(8,128)S(1)} %get-tuple-element.19), channel_id=1, source_target_pairs={{0,12},{1,13},{2,14},{3,15},{4,8},{5,9},{6,10},{7,11},{8,4},{9,5},... | collective-permute-start | bytes 294920 | tf_op jit(solution)/shard_map/ppermute | solution.py:162
  23.5 22.4 %collective-permute-start.5 = (f32[192,128]{1,0:T(8,128)S(1)}, f32[192,128]{1,0:T(8,128)S(1)}, u32[]{:S(2)}, u32[]{:S(2)}) collective-permute-start(f32[192,128]{1,0:T(8,128)S(1)} %get-tuple-element.20), channel_id=1, source_target_pairs={{0,4},{1,5},{2,6},{3,7},{4,0},{5,1},{6,2},{7,3},{8,12},{9,13},{10,... | collective-permute-start | bytes 294920 | tf_op jit(solution)/shard_map/ppermute | solution.py:162
  23.5 1.2 %collective-permute-start.6 = (f32[2,128]{1,0:T(2,128)S(1)}, f32[2,128]{1,0:T(2,128)S(1)}, u32[]{:S(2)}, u32[]{:S(2)}) collective-permute-start(f32[2,128]{1,0:T(2,128)S(1)} %get-tuple-element.21), channel_id=1, source_target_pairs={{0,16},{16,0},{1,17},{17,1},{2,18},{18,2},{3,19},{19,3},{4,20},{20... | collective-permute-start | bytes 3080 | tf_op jit(solution)/shard_map/ppermute | solution.py:154
  25.3 20.5 %all-to-all-start = ((f32[64,2,128]{2,1,0:T(2,128)}), f32[64,2,128]{2,1,0:T(2,128)S(1)}, u32[]{:S(2)}, u32[]{:S(2)}) async-start(f32[64,2,128]{2,1,0:T(2,128)} %broadcast_in_dim.2), calls=%async_computation | async-start | bytes 131072 | tf_op jit(solution)/shard_map/all_to_all | solution.py:169

commit v4 on v3

--- a/solution.py
+++ b/solution.py
@@ -29,6 +29,18 @@
 
 def second_stage(d):
     return [(index(z, k, y, x), index(z, k, y ^ (d * (1 - k)), x ^ (d * k))) for z, k, y, x in PLACES]
+
+
+def classes(key):
+    found = {}
+    for place in PLACES:
+        found.setdefault(key(*place), []).append(index(*place))
+    return [sorted(found[name], key=FIRST) for name in sorted(found)]
+
+
+FIRST = lambda n: (n not in (index(3, 0, 2, 1), index(1, 1, 1, 2)), n)
+HOPS = []
+GROUPS = classes(lambda z, k, y, x: k)
 
 
 def partial_sums(place, kernel, labels, *refs):
@@ -153,6 +165,9 @@
     )(place, kernel, labels)
     other = lax.ppermute(totals, "k", [(0, 1), (1, 0)])
     chip = totals + other
+    for hop in HOPS:
+        other = lax.ppermute(chip, AXES, hop)
+        chip = chip + other
     moved = [parts[0]] + [early(parts[s], s) for s in (1, 3, 2)]
     halves = pl.pallas_call(
         stage_sum, out_shape=[small] * 4, in_specs=[vmem()] * 4, out_specs=[vmem()] * 4
@@ -167,9 +182,14 @@
         out_specs=vmem(),
     )(labels, near(halves[0]))
     shares = lax.all_to_all(
-        jnp.broadcast_to(chip[None], (64, 2, SLICE)), ("z", "y", "x"), 0, 0, tiled=True
+        jnp.broadcast_to(chip[None], (len(GROUPS[0]), 2, SLICE)),
+        AXES,
+        0,
+        0,
+        axis_index_groups=GROUPS,
+        tiled=True,
     )
-    shares = shares.reshape(16, 8, SLICE)
+    shares = shares.reshape(len(GROUPS[0]) // 4, 8, SLICE)
     distance, objective = pl.pallas_call(
         finish,
         out_shape=[

time: 46.9 us -> 44.4 us (0.947)
  the two profiles are of different devices: /device:TPU:0 before, /device:TPU:1 now
where the time goes in v4:
time: 44.4 us; the launch traced here: 44.2 us
  starting transfers between devices  22 us (50%)
  waiting for transfers between devices  14.5 us (33%)
  Pallas kernels  6.37 us (14%)
  between operations  0.68 us (2%)
  local copies, waits for them, and re-layouts  0.65 us (1%)
    all_to_all x1, starting transfers between devices, shards(): lax.all_to_all(jnp.broadcast_to(chip[None], (len(GROUPS[0]), 2, SLICE)),...  11.1 us
    ppermute x3, waiting for transfers between devices, early(): return lax.ppermute(part, AXES, first_stage(s))  9.66 us
    ppermute x3, starting transfers between devices, early(): return lax.ppermute(part, AXES, first_stage(s))  4.82 us
    all_to_all x1, waiting for transfers between devices, shards(): lax.all_to_all(jnp.broadcast_to(chip[None], (len(GROUPS[0]), 2, SLICE)),...  3.97 us
    pallas_call x1, Pallas kernels, shards(): pl.pallas_call(partial_sums, out_shape=[block] * 4 + [pltpu.VMEM((2, SLIC...  3.53 us
    ppermute x3, starting transfers between devices, shards(): last.append(lax.ppermute(halves[s], AXES, second_stage(s)))  3.45 us
    ppermute x1, starting transfers between devices, shards(): other = lax.ppermute(totals, 'k', [(0, 1), (1, 0)])  2.66 us
    pallas_call x1, Pallas kernels, shards(): pl.pallas_call(tally, out_shape=pltpu.VMEM((ITERS, CLUSTERS, SLICE), jnp....  1.91 us
  transfers between devices with their start and end apart: 8, of which 5 were waited for; matrix products, arithmetic and copies ran while one was open for 1% of the time, Pallas kernels for 4%

profile of v4, /device:TPU:1, one launch (start us, length us, event | category | flops | bytes accessed | tf_op | source)
XLA Modules:
  0.0 44.2 jit_solution(16713716509531047205)
XLA Ops:
  0.6 3.5 %shard_map.41 = (f32[4,192,128]{2,1,0:T(8,128)S(1)}, f32[4,192,128]{2,1,0:T(8,128)S(1)}, f32[4,192,128]{2,1,0:T(8,128)S(1)}, f32[4,192,128]{2,1,0:T(8,128)S(1)}, f32[2,128]{1,0:T(2,128)S(1)}) custom-call(s32[1]{0:T(128)} %bitcast.place, bf16[2048,1024]{1,0:T(8,128)(2,1)} %kernel.1, s32[3,16384]{1,0:T(4,128)} %labels.3), custom_call_target="tpu_custom_call" | custom-call | tf_op jit(solution)/shard_map/pallas_call | solution.py:150
  4.2 2.2 %collective-permute-start = (f32[4,192,128]{2,1,0:T(8,128)S(1)}, f32[4,192,128]{2,1,0:T(8,128)S(1)}, u32[]{:S(2)}, u32[]{:S(2)}) collective-permute-start(f32[4,192,128]{2,1,0:T(8,128)S(1)} %get-tuple-element.14), channel_id=1, source_target_pairs={{0,1},{1,0},{2,3},{3,2},{4,5},{5,4},{6,7},{7,6},{8,9},{9,8},{10,11... | collective-permute-start | bytes 1179656 | tf_op jit(solution)/shard_map/ppermute | solution.py:138
  6.4 1.9 %collective-permute-start.1 = (f32[4,192,128]{2,1,0:T(8,128)S(1)}, f32[4,192,128]{2,1,0:T(8,128)S(1)}, u32[]{:S(2)}, u32[]{:S(2)}) collective-permute-start(f32[4,192,128]{2,1,0:T(8,128)S(1)} %get-tuple-element.15), channel_id=1, source_target_pairs={{0,3},{1,2},{2,1},{3,0},{4,7},{5,6},{6,5},{7,4},{8,11},{9,10},{10,... | collective-permute-start | bytes 1179656 | tf_op jit(solution)/shard_map/ppermute | solution.py:138
  8.3 0.7 %collective-permute-start.2 = (f32[4,192,128]{2,1,0:T(8,128)S(1)}, f32[4,192,128]{2,1,0:T(8,128)S(1)}, u32[]{:S(2)}, u32[]{:S(2)}) collective-permute-start(f32[4,192,128]{2,1,0:T(8,128)S(1)} %get-tuple-element.16), channel_id=1, source_target_pairs={{0,2},{1,3},{2,0},{3,1},{4,6},{5,7},{6,4},{7,5},{8,10},{9,11},{10,... | collective-permute-start | bytes 1179656 | tf_op jit(solution)/shard_map/ppermute | solution.py:138
  9.0 2.8 %collective-permute-done.b = f32[4,192,128]{2,1,0:T(8,128)S(1)} collective-permute-done((f32[4,192,128]{2,1,0:T(8,128)S(1)}, f32[4,192,128]{2,1,0:T(8,128)S(1)}, u32[]{:S(2)}, u32[]{:S(2)}) %collective-permute-start) | collective-permute-done | bytes 393248 | tf_op jit(solution)/shard_map/ppermute | solution.py:138
  11.8 5.4 %collective-permute-done.1.c = f32[4,192,128]{2,1,0:T(8,128)S(1)} collective-permute-done((f32[4,192,128]{2,1,0:T(8,128)S(1)}, f32[4,192,128]{2,1,0:T(8,128)S(1)}, u32[]{:S(2)}, u32[]{:S(2)}) %collective-permute-start.1) | collective-permute-done | bytes 393248 | tf_op jit(solution)/shard_map/ppermute | solution.py:138
  17.2 1.5 %collective-permute-done.2.d = f32[4,192,128]{2,1,0:T(8,128)S(1)} collective-permute-done((f32[4,192,128]{2,1,0:T(8,128)S(1)}, f32[4,192,128]{2,1,0:T(8,128)S(1)}, u32[]{:S(2)}, u32[]{:S(2)}) %collective-permute-start.2) | collective-permute-done | bytes 393248 | tf_op jit(solution)/shard_map/ppermute | solution.py:138
  18.7 0.1 shard_map.42
  18.7 2.6 %collective-permute-start.3 = (f32[192,128]{1,0:T(8,128)S(1)}, f32[192,128]{1,0:T(8,128)S(1)}, u32[]{:S(2)}, u32[]{:S(2)}) collective-permute-start(f32[192,128]{1,0:T(8,128)S(1)} %get-tuple-element.18), channel_id=1, source_target_pairs={{0,8},{1,9},{2,10},{3,11},{4,12},{5,13},{6,14},{7,15},{8,0},{9,1},... | collective-permute-start | bytes 294920 | tf_op jit(solution)/shard_map/ppermute | solution.py:177
  21.3 0.9 %collective-permute-start.4 = (f32[192,128]{1,0:T(8,128)S(1)}, f32[192,128]{1,0:T(8,128)S(1)}, u32[]{:S(2)}, u32[]{:S(2)}) collective-permute-start(f32[192,128]{1,0:T(8,128)S(1)} %get-tuple-element.19), channel_id=1, source_target_pairs={{0,12},{1,13},{2,14},{3,15},{4,8},{5,9},{6,10},{7,11},{8,4},{9,5},... | collective-permute-start | bytes 294920 | tf_op jit(solution)/shard_map/ppermute | solution.py:177
  22.2 0.0 collective-permute-start.5
  22.2 2.7 %collective-permute-start.6 = (f32[2,128]{1,0:T(2,128)S(1)}, f32[2,128]{1,0:T(2,128)S(1)}, u32[]{:S(2)}, u32[]{:S(2)}) collective-permute-start(f32[2,128]{1,0:T(2,128)S(1)} %get-tuple-element.21), channel_id=1, source_target_pairs={{0,16},{16,0},{1,17},{17,1},{2,18},{18,2},{3,19},{19,3},{4,20},{20... | collective-permute-start | bytes 3080 | tf_op jit(solution)/shard_map/ppermute | solution.py:166
  24.9 0.8 %collective-permute-done.6 = f32[2,128]{1,0:T(2,128)S(1)} collective-permute-done((f32[2,128]{1,0:T(2,128)S(1)}, f32[2,128]{1,0:T(2,128)S(1)}, u32[]{:S(2)}, u32[]{:S(2)}) %collective-permute-start.6) | collective-permute-done | bytes 1056 | tf_op jit(solution)/shard_map/ppermute | solution.py:166
  25.7 0.6 %broadcast_in_dim.2 = f32[64,2,128]{2,1,0:T(2,128)} broadcast(f32[2,128]{1,0:T(2,128)S(1)} %add.15), dimensions={1,2} | broadcast | bytes 66560 | tf_op jit(solution)/shard_map/broadcast_in_dim | solution.py:185
  26.3 11.1 %all-to-all-start = ((f32[64,2,128]{2,1,0:T(2,128)}), f32[64,2,128]{2,1,0:T(2,128)S(1)}, u32[]{:S(2)}, u32[]{:S(2)}) async-start(f32[64,2,128]{2,1,0:T(2,128)} %broadcast_in_dim.2), calls=%async_computation | async-start | bytes 131072 | tf_op jit(solution)/shard_map/all_to_all | solution.py:184
  37.4 1.9 %shard_map.43.counts = f32[3,64,128]{2,1,0:T(8,128)S(1)} custom-call(s32[3,16384]{1,0:T(4,128)} %labels.3, f32[192,128]{1,0:T(8,128)S(1)} %get-tuple-element.17.after.a), custom_call_target="tpu_custom_call" | custom-call | tf_op jit(solution)/shard_map/pallas_call | solution.py:178
  39.3 4.0 %all-to-all-done = f32[64,2,128]{2,1,0:T(2,128)S(1)} async-done(((f32[64,2,128]{2,1,0:T(2,128)}), f32[64,2,128]{2,1,0:T(2,128)S(1)}, u32[]{:S(2)}, u32[]{:S(2)}) %all-to-all-start) | async-done | bytes 65568 | tf_op jit(solution)/shard_map/all_to_all | solution.py:184
  43.3 0.0 collective-permute-done.3.b
  43.3 0.0 collective-permute-done.4.c
  43.3 0.0 collective-permute-done.5.d
  43.3 0.9 %shard_map.44 = (f32[3,64,128]{2,1,0:T(8,128)}, f32[3]{0:T(128)}) custom-call(f32[192,128]{1,0:T(8,128)S(1)} %get-tuple-element.17.after.a, f32[192,128]{1,0:T(8,128)S(1)} %collective-permute-done.3.b, f32[192,128]{1,0:T(8,128)S(1)} %collective-permute-done.4.c, f32[192,128]{1,0:T(8,128)S(1)} %collective-permute-done.5.d, ...), custom_call_target="tpu_custom_call" | custom-call | tf_op jit(solution)/shard_map/pallas_call | solution.py:193
  (1 shorter events, 0.0 us)
Async XLA Ops:
  4.2 7.7 %collective-permute-start = (f32[4,192,128]{2,1,0:T(8,128)S(1)}, f32[4,192,128]{2,1,0:T(8,128)S(1)}, u32[]{:S(2)}, u32[]{:S(2)}) collective-permute-start(f32[4,192,128]{2,1,0:T(8,128)S(1)} %get-tuple-element.14), channel_id=1, source_target_pairs={{0,1},{1,0},{2,3},{3,2},{4,5},{5,4},{6,7},{7,6},{8,9},{9,8},{10,11... | collective-permute-start | bytes 1179656 | tf_op jit(solution)/shard_map/ppermute | solution.py:138
  6.4 10.8 %collective-permute-start.1 = (f32[4,192,128]{2,1,0:T(8,128)S(1)}, f32[4,192,128]{2,1,0:T(8,128)S(1)}, u32[]{:S(2)}, u32[]{:S(2)}) collective-permute-start(f32[4,192,128]{2,1,0:T(8,128)S(1)} %get-tuple-element.15), channel_id=1, source_target_pairs={{0,3},{1,2},{2,1},{3,0},{4,7},{5,6},{6,5},{7,4},{8,11},{9,10},{10,... | collective-permute-start | bytes 1179656 | tf_op jit(solution)/shard_map/ppermute | solution.py:138
  8.3 10.4 %collective-permute-start.2 = (f32[4,192,128]{2,1,0:T(8,128)S(1)}, f32[4,192,128]{2,1,0:T(8,128)S(1)}, u32[]{:S(2)}, u32[]{:S(2)}) collective-permute-start(f32[4,192,128]{2,1,0:T(8,128)S(1)} %get-tuple-element.16), channel_id=1, source_target_pairs={{0,2},{1,3},{2,0},{3,1},{4,6},{5,7},{6,4},{7,5},{8,10},{9,11},{10,... | collective-permute-start | bytes 1179656 | tf_op jit(solution)/shard_map/ppermute | solution.py:138
  18.7 24.6 %collective-permute-start.3 = (f32[192,128]{1,0:T(8,128)S(1)}, f32[192,128]{1,0:T(8,128)S(1)}, u32[]{:S(2)}, u32[]{:S(2)}) collective-permute-start(f32[192,128]{1,0:T(8,128)S(1)} %get-tuple-element.18), channel_id=1, source_target_pairs={{0,8},{1,9},{2,10},{3,11},{4,12},{5,13},{6,14},{7,15},{8,0},{9,1},... | collective-permute-start | bytes 294920 | tf_op jit(solution)/shard_map/ppermute | solution.py:177
  21.3 22.0 %collective-permute-start.4 = (f32[192,128]{1,0:T(8,128)S(1)}, f32[192,128]{1,0:T(8,128)S(1)}, u32[]{:S(2)}, u32[]{:S(2)}) collective-permute-start(f32[192,128]{1,0:T(8,128)S(1)} %get-tuple-element.19), channel_id=1, source_target_pairs={{0,12},{1,13},{2,14},{3,15},{4,8},{5,9},{6,10},{7,11},{8,4},{9,5},... | collective-permute-start | bytes 294920 | tf_op jit(solution)/shard_map/ppermute | solution.py:177
  22.2 21.1 %collective-permute-start.5 = (f32[192,128]{1,0:T(8,128)S(1)}, f32[192,128]{1,0:T(8,128)S(1)}, u32[]{:S(2)}, u32[]{:S(2)}) collective-permute-start(f32[192,128]{1,0:T(8,128)S(1)} %get-tuple-element.20), channel_id=1, source_target_pairs={{0,4},{1,5},{2,6},{3,7},{4,0},{5,1},{6,2},{7,3},{8,12},{9,13},{10,... | collective-permute-start | bytes 294920 | tf_op jit(solution)/shard_map/ppermute | solution.py:177
  22.2 3.5 %collective-permute-start.6 = (f32[2,128]{1,0:T(2,128)S(1)}, f32[2,128]{1,0:T(2,128)S(1)}, u32[]{:S(2)}, u32[]{:S(2)}) collective-permute-start(f32[2,128]{1,0:T(2,128)S(1)} %get-tuple-element.21), channel_id=1, source_target_pairs={{0,16},{16,0},{1,17},{17,1},{2,18},{18,2},{3,19},{19,3},{4,20},{20... | collective-permute-start | bytes 3080 | tf_op jit(solution)/shard_map/ppermute | solution.py:166
  26.3 17.0 %all-to-all-start = ((f32[64,2,128]{2,1,0:T(2,128)}), f32[64,2,128]{2,1,0:T(2,128)S(1)}, u32[]{:S(2)}, u32[]{:S(2)}) async-start(f32[64,2,128]{2,1,0:T(2,128)} %broadcast_in_dim.2), calls=%async_computation | async-start | bytes 131072 | tf_op jit(solution)/shard_map/all_to_all | solution.py:184
